TPU v7x, 128 devices: a whole 4x4x4 slice. The times are simulated.
128 devices in a mesh: ta: 64 (over y, x, z), gz: 2 (over core).
Axes of the slice: x: 4, y: 4, z: 4, core: 2. Of those that a mesh axis runs over, the one named last changes fastest.
Arguments:
- propagator: float32 [2, 12, 12, 64, 13824], P(None, None, None, 'ta', 'gz'), may hold values from -6 to 6
- backward: float32 [2, 12, 12, 64, 13824], P(None, None, None, 'ta', 'gz'), may hold values from -6 to 6
- sink_time: int32 [1], replicated, may hold values from 0 to 63
- source_position: int32 [3], replicated, may hold values from 0 to 23
- momenta: int32 [27, 3], replicated, may hold values from -3 to 3
- gamma_table: int32 [16], replicated, may hold values from 0 to 15, each once
Outputs:
- correlator: float32 [2, 64, 16, 27], P(None, 'ta', 'gz')
Inputs may be any that keep to these rules, and one draw needn't show every extreme that they name: `gamma_table`: each of 0 to 15 appears exactly once.
All inputs are finite; a program needn't handle non-finite values.
Results may differ from a plain program's by a relative error of at most 0.00007.
Values sent between devices are 32-bit elements; how exact they have to be, the bound alone decides.
No kernel may reach another device: no remote copies, remote signals or barrier semaphores. Data moves between devices by JAX's collectives and lax.ppermute only.
A program may use at most 192 MiB of HBM per device.

v0:
```python
import math

import jax
import jax.numpy as jnp
import numpy as np
from jax import lax
from jax.experimental import pallas as pl
from jax.experimental.pallas import tpu as pltpu
from jax.sharding import PartitionSpec as P


L = 24
NP = 27
ROWS = 54
A_START = (0, 14, 28, 42)
B_START = (8, 22, 36, 48)
F32 = jnp.float32
BF16 = jnp.bfloat16


def pair_index(m, n):
    m, n = min(m, n), max(m, n)
    return m * 12 - m * (m - 1) // 2 + (n - m)


def gamma_weights():
    paulis = [
        np.eye(2),
        np.array([[0.0, 1.0], [1.0, 0.0]]),
        np.array([[0.0, -1j], [1j, 0.0]]),
        np.array([[1.0, 0.0], [0.0, -1.0]]),
    ]
    matrices = np.stack([np.kron(paulis[number // 4], paulis[number % 4]) for number in range(16)])
    flat = matrices.reshape(16, 16) / (72.0 * math.sqrt(L * L * L))
    top = np.concatenate([flat.real, -flat.imag], axis=1)
    low = np.concatenate([flat.imag, flat.real], axis=1)
    return np.concatenate([top, low]).astype(np.float32)


PIECES = 4


def block_copies(field, start, rows, buf, sems):
    span = 288 // PIECES
    return [
        pltpu.make_async_copy(
            field.at[pl.ds(i * span, span), pl.ds(start, rows), 0, :],
            buf.at[pl.ds(i * span, span), pl.ds(0, rows), :],
            sems.at[i],
        )
        for i in range(PIECES)
    ]


def source_block(buf, sums, write):
    for e in range(144):
        sums[e] = buf[e] + buf[144 + e]
    for mt in range(0, 12, 3):
        for nt in range(mt, 12, 3):
            pairs = [(m, n) for m in range(mt, mt + 3) for n in range(nt, nt + 3) if m <= n]
            acc = {}
            for k in range(12):
                rows = sorted({m for m, _ in pairs} | {n for _, n in pairs})
                re = {m: buf[m * 12 + k] for m in rows}
                im = {m: buf[144 + m * 12 + k] for m in rows}
                su = {m: sums[m * 12 + k] for m in rows}
                for m, n in pairs:
                    new = (re[m] * re[n], im[m] * im[n], su[m] * su[n])
                    acc[m, n] = new if k == 0 else tuple(a + b for a, b in zip(acc[m, n], new))
            for m, n in pairs:
                p1, p2, p3 = acc[m, n]
                write(pair_index(m, n), 0.125 * (p1 - p2), 0.125 * (p3 - p1 - p2))


def source_kernel(blocks, sink_ref, field, *refs):
    outs = refs[: len(blocks)]
    bufs, stage, sums, sems, out_sems = refs[len(blocks) :]

    @pl.when(lax.axis_index("ta") == sink_ref[0])
    def _():
        def copies_in(i):
            quarter, half = blocks[i]
            start = (A_START, B_START)[half][quarter]
            return block_copies(field, start, 8 - 2 * half, bufs.at[i], sems.at[i])

        def copy_out(i):
            rows = 40 * (8 - 2 * blocks[i][1])
            return pltpu.make_async_copy(stage.at[i, :, pl.ds(0, rows), :], outs[i], out_sems.at[i])

        for i in range(min(2, len(blocks))):
            for copy in copies_in(i):
                copy.start()
        for i, (_, half) in enumerate(blocks):
            for copy in copies_in(i):
                copy.wait()
            if i + 2 < len(blocks):
                for copy in copies_in(i + 2):
                    copy.start()

            def write(u, re, im, i=i, rows=8 - 2 * half):
                for e, v in ((u, re), (78 + u, im)):
                    first = e % 39 * rows
                    stage[i, e // 39, first : first + rows, :] = v[:rows]

            source_block(bufs.at[i], sums, write)
            copy_out(i).start()
        for i in range(len(blocks)):
            copy_out(i).wait()


def source(blocks, sink_time, field):
    count = len(blocks)

    def kernel(*refs):
        source_kernel(blocks, *refs)

    anywhere = pl.BlockSpec(memory_space=pl.ANY)
    return pl.pallas_call(
        kernel,
        in_specs=[pl.BlockSpec(memory_space=pltpu.SMEM), anywhere],
        out_specs=[anywhere] * count,
        out_shape=[jax.ShapeDtypeStruct((4, 40 * (8 - 2 * half), 128), F32) for _, half in blocks],
        scratch_shapes=[
            pltpu.VMEM((count, 288, 8, 128), F32),
            pltpu.VMEM((count, 4, 320, 128), F32),
            pltpu.VMEM((144, 8, 128), F32),
            pltpu.SemaphoreType.DMA((count, PIECES)),
            pltpu.SemaphoreType.DMA((count,)),
        ],
    )(sink_time, field)


STRIDE = {"y": 16, "x": 4, "z": 1}
AXES = ((("x", 1), ("y", 1), ("z", 1)), (("y", -1), ("z", -1), ("x", -1)))
UNIT = ((1, 0, 0), (0, 1, 0), (0, 0, 1))
TWICE = ((2, 0, 0), (0, 2, 0), (0, 0, 2))
DIAGONAL = ((1, 1, 1), (2, 2, 2), (3, 3, 3))


def moved(vector):
    pairs = []
    for place in range(64):
        for core in range(2):
            target = place
            for (axis, sign), step in zip(AXES[core], vector):
                digit = place // STRIDE[axis] % 4
                target += ((digit + sign * step) % 4 - digit) * STRIDE[axis]
            pairs.append((2 * place + core, 2 * target + core))
    return pairs


def shift(value, vector):
    return lax.ppermute(value, ("ta", "gz"), moved(vector))


def relative(there):
    here, core = lax.axis_index("ta"), lax.axis_index("gz")
    digits = {"y": 4, "x": 2, "z": 0}
    steps = {a: (here >> n) - (there >> n) for a, n in digits.items()}
    out = []
    for i in range(3):
        (a0, s0), (a1, s1) = AXES[0][i], AXES[1][i]
        out.append(jnp.where(core == 0, s0 * steps[a0], s1 * steps[a1]) & 3)
    return out


def labels_at(u, v, w):
    low, high = (u ^ w) & 1, (v ^ w) & 1
    c = low + 2 * high
    hu = (u - (low & (1 - high))) & 3
    hv = (v - (high & (1 - low))) & 3
    hw = (w - (low & high)) & 3
    d_low, d_high = (hu >> 1) ^ (hw >> 1), (hv >> 1) ^ (hw >> 1)
    copy = (hu - 2 * (d_low & (1 - d_high))) & 3
    return c, d_low + 2 * d_high, copy


def received(there, k):
    u, v, w = relative(there)
    du, dv, dw = (0, 0, 0) if k == 0 else UNIT[k - 1]
    c, d, _ = labels_at((u - du) & 3, (v - dv) & 3, (w - dw) & 3)
    return c, d


def pick(index, sources):
    value = sources[-1]
    for i in range(len(sources) - 2, -1, -1):
        value = jnp.where(index == i, sources[i], value)
    return value


def spread(upper, lower, there, ready):
    c, d, copy = labels_at(*relative(there))
    upper = [upper[0]] + [shift(upper[k], UNIT[k - 1]) for k in (1, 2, 3)]
    lower = [lower[0]] + [shift(lower[k], UNIT[k - 1]) for k in (1, 2, 3)]
    c, ready = lax.optimization_barrier((c, ready))
    groups = [
        jnp.concatenate([pick(c, [a[g] for a in upper]), pick(c, [a[g] for a in lower])])
        for g in range(4)
    ]
    got = [shift(groups[k], TWICE[k - 1]) for k in (1, 2, 3)]
    piece = pick(d, [groups[0]] + got)
    got = [shift(piece, DIAGONAL[k - 1]) for k in (1, 2, 3)]
    piece = pick(copy, [piece] + got)
    groups = [piece] + [shift(piece, TWICE[k - 1]) for k in (1, 2, 3)]
    lower = jnp.stack([g[320:] for g in groups])
    lower_got = [shift(lower, UNIT[k]) for k in range(3)]
    upper = jnp.stack([g[:320] for g in groups])
    upper_got = [shift(upper, UNIT[k]) for k in range(3)]
    return [upper] + upper_got, [lower] + lower_got, ready


def contract_block(rows, b, slots, s_buf, h_buf, g_buf, sig, s_sum, h_sum, macc, mout):
    for u in range(78):
        part = []
        for e in (u, 78 + u):
            v = g_buf[b, slots[e // 39], e % 39 * rows : e % 39 * rows + rows, :]
            sig[(e // 78) * 78 + u, 0:rows, :] = v
            part.append(v)
        sig[156 + u, 0:rows, :] = part[0] + part[1]
    for e in range(144):
        s_sum[e] = s_buf[b, e] + s_buf[b, 144 + e]
        h_sum[e] = h_buf[b, e] + h_buf[b, 144 + e]

    def spin(alpha, carry):
        base = alpha * 36
        for nt in range(0, 12, 3):
            acc = {}
            for m in range(12):
                h = [
                    (h_buf[b, base + a * 12 + m], h_buf[b, base + (144 + a * 12 + m)], h_sum[base + a * 12 + m])
                    for a in range(3)
                ]
                for n in range(nt, nt + 3):
                    u = pair_index(m, n)
                    g = (sig[u], sig[78 + u], sig[156 + u])
                    for a in range(3):
                        new = tuple(x * y for x, y in zip(h[a], g))
                        acc[a, n] = new if m == 0 else tuple(x + y for x, y in zip(acc[a, n], new))
            conj = {}
            for key, (p1, p2, p3) in acc.items():
                u_, w_ = p1 - p2, p1 + p2 - p3
                conj[key] = (u_, w_, u_ + w_)
            for beta in range(4):
                q = None
                for (a, n), t in conj.items():
                    e = (3 * beta + a) * 12 + n
                    s = (s_buf[b, e], s_buf[b, 144 + e], s_sum[e])
                    new = tuple(x * y for x, y in zip(s, t))
                    q = new if q is None else tuple(x + y for x, y in zip(q, new))
                if nt > 0:
                    q = tuple(q[i] + macc[beta, i] for i in range(3))
                if nt < 9:
                    for i in range(3):
                        macc[beta, i] = q[i]
                else:
                    mout[alpha * 4 + beta] = q[0] - q[1]
                    mout[16 + alpha * 4 + beta] = q[2] - q[0] - q[1]
        return carry

    lax.fori_loop(0, 4, spin, 0)


def project(rows, mout, phases, total):
    for pair in range(rows // 2):
        wide = jnp.concatenate([mout[:, 2 * pair, :], mout[:, 2 * pair + 1, :]], axis=1)
        high = wide.astype(BF16)
        low = (wide - high.astype(F32)).astype(BF16)
        total += lax.dot_general(
            jnp.concatenate([high, low], axis=0),
            phases[pair],
            (((1,), (1,)), ((), ())),
            preferred_element_type=F32,
        )
    return total


def currents(weights, total):
    total = total[:32] + total[32:]
    total = total[:, :64] + total[:, 64:]
    cosine, sine = total[:, :28], total[:, 32:60]
    re = cosine[:16] - sine[16:]
    im = sine[:16] + cosine[16:]
    result = jnp.dot(
        weights,
        jnp.concatenate([re, im], axis=0),
        precision=lax.Precision.HIGHEST,
        preferred_element_type=F32,
    )
    return tuple(result[8 * i : 8 * i + 8] for i in range(4))


def contract_kernel(blocks, more, last, sink_ref, prop, back, phases_a, phases_b, *refs):
    nb = len(blocks)
    fields, refs = refs[:nb], refs[nb:]
    if more:
        before, refs = refs[0], refs[1:]
    if last:
        weights, gammas, keep_ref, send_ref = refs[:4]
        refs = refs[4:]
    else:
        out_ref, refs = refs[0], refs[1:]
    s_buf, h_buf, g_buf, p_buf, sig, s_sum, h_sum, macc, mout, acc, numbers, sems = refs

    def copies(b):
        half = blocks[b][1]
        rows = 8 - 2 * half
        starts, phases = ((A_START, phases_a), (B_START, phases_b))[half]
        start = jnp.int32(starts[3])
        for i in range(3):
            start = jnp.where(numbers[b, 0] == i, starts[i], start)
        return [
            pltpu.make_async_copy(
                fields[b], g_buf.at[b, :, pl.ds(0, 40 * rows), :], sems.at[b, 2 * PIECES]
            ),
            *block_copies(back, start, rows, h_buf.at[b], sems.at[b, pl.ds(0, PIECES)]),
            *block_copies(prop, start, rows, s_buf.at[b], sems.at[b, pl.ds(PIECES, PIECES)]),
            pltpu.make_async_copy(
                phases.at[numbers[b, 0]], p_buf.at[b, pl.ds(0, rows // 2)], sems.at[b, 2 * PIECES + 1]
            ),
        ]

    def on(b, action):
        for i in range(nb):

            @pl.when(b == i)
            def _():
                for copy in copies(i):
                    action(copy)

    for b, (k, _) in enumerate(blocks):
        numbers[b, 0], numbers[b, 1] = received(sink_ref[0], k)
    for copy in copies(0):
        copy.start()
    acc[...] = before[...] if more else jnp.zeros_like(acc)
    for half in (0, 1):
        chosen = [b for b in range(nb) if blocks[b][1] == half]
        rows = 8 - 2 * half

        def block(b, carry, rows=rows):
            on(b, lambda copy: copy.wait())
            on(b + 1, lambda copy: copy.start())
            slots = [numbers[b, 1] ^ g for g in range(4)]
            contract_block(rows, b, slots, s_buf, h_buf, g_buf, sig, s_sum, h_sum, macc, mout)
            acc[...] = project(rows, mout, p_buf.at[b], acc[...])
            return carry

        if chosen:
            lax.fori_loop(chosen[0], chosen[-1] + 1, block, 0)
    if last:
        mout[0, :, :28], mout[1, :, :28], mout[2, :, :28], mout[3, :, :28] = currents(weights[...], acc[...])
        core = lax.axis_index("gz")
        for i in range(16):
            out = (keep_ref, send_ref)[i // 8]
            row = gammas[(i + 8 * core) & 15]
            for part in range(2):
                out[part, pl.ds(i % 8, 1), :] = mout[2 * part + (row >> 3), pl.ds(row & 7, 1), :NP]
    else:
        out_ref[...] = acc[...]


def contract(blocks, sink_time, prop, back, phases, fields, before=None, weights=None, gammas=None):
    nb = len(blocks)
    more, last = before is not None, weights is not None

    def kernel(*refs):
        contract_kernel(blocks, more, last, *refs)

    anywhere = pl.BlockSpec(memory_space=pl.ANY)
    vmem = pl.BlockSpec(memory_space=pltpu.VMEM)
    smem = pl.BlockSpec(memory_space=pltpu.SMEM)
    if last:
        out_shape = [jax.ShapeDtypeStruct((2, 8, NP), F32)] * 2
    else:
        out_shape = [jax.ShapeDtypeStruct((64, 128), F32)]
    return pl.pallas_call(
        kernel,
        in_specs=[smem] + [anywhere] * (4 + nb) + [vmem] * more + [vmem, smem] * last,
        out_specs=[vmem] * len(out_shape),
        out_shape=out_shape,
        scratch_shapes=[
            pltpu.VMEM((nb, 288, 8, 128), F32),
            pltpu.VMEM((nb, 288, 8, 128), F32),
            pltpu.VMEM((nb, 4, 320, 128), F32),
            pltpu.VMEM((nb, 4, 128, 256), BF16),
            pltpu.VMEM((234, 8, 128), F32),
            pltpu.VMEM((144, 8, 128), F32),
            pltpu.VMEM((144, 8, 128), F32),
            pltpu.VMEM((4, 3, 8, 128), F32),
            pltpu.VMEM((32, 8, 128), F32),
            pltpu.VMEM((64, 128), F32),
            pltpu.SMEM((nb, 2), jnp.int32),
            pltpu.SemaphoreType.DMA((nb, 2 * PIECES + 2)),
        ],
    )(sink_time, prop, back, *phases, *fields, *([before] if more else []), *([weights, gammas] if last else []))


def cosine_of(wave):
    wave = wave - 24.0 * jnp.floor((wave + 0.5) * (1.0 / 24.0))
    t = (jnp.abs(wave - 12.0) - 6.0) * (math.pi / 12.0)
    t2 = t * t
    value = t2 * (1.0 / 6227020800.0) - 1.0 / 39916800.0
    for k in (362880.0, -5040.0, 120.0, -6.0):
        value = value * t2 + 1.0 / k
    return t + t * (t2 * value)


def site_places():
    out = np.zeros((28, 8, 256), np.float32)
    lane = np.arange(256)
    number = 0
    for starts, pairs in ((A_START, 4), (B_START, 3)):
        for q in range(4):
            for pair in range(pairs):
                site = (starts[q] + 2 * pair) * 128 + lane
                out[number, 0], out[number, 1], out[number, 2] = site // L % L, site % L, site // (L * L)
                out[number, 3] = 0.0 if (pairs, q, pair) == (3, 3, 0) else 1.0
                number += 1
    return out


def phase_kernel(source_ref, momenta, places, out_a, out_b, wide):
    core = lax.axis_index("gz").astype(F32)
    table = momenta[...].astype(F32)
    table = jnp.concatenate([table, jnp.zeros((32 - NP, 3), F32)], axis=0)
    for i in range(3):
        column = jnp.broadcast_to(table[:, i : i + 1], (32, 256))
        wide[i, :32, :] = column
        wide[i, 32:, :] = column
    origin = [source_ref[i].astype(F32) for i in range(3)]
    origin[2] = origin[2] - 12.0 * core
    turn = jnp.where(lax.broadcasted_iota(jnp.int32, (64, 256), 0) < 32, 0.0, 6.0)

    def pair(number, out, q, p):
        wave = turn
        for i in range(3):
            wave = wave + wide[i] * (places[number, i : i + 1, :] - origin[i])
        value = cosine_of(wave) * places[number, 3:4, :]
        high = value.astype(BF16)
        out[q, p, :64, :] = high
        out[q, p, 64:, :] = (value - high.astype(F32)).astype(BF16)

    def step_a(n, carry):
        pair(n, out_a, n >> 2, n & 3)
        return carry

    lax.fori_loop(0, 16, step_a, 0)
    for q in range(4):

        def step_b(p, carry, q=q):
            pair(16 + 3 * q + p, out_b, q, p)
            return carry

        lax.fori_loop(0, 3, step_b, 0)


def phase_blocks(source_position, momenta):
    vmem = pl.BlockSpec(memory_space=pltpu.VMEM)
    return pl.pallas_call(
        phase_kernel,
        in_specs=[pl.BlockSpec(memory_space=pltpu.SMEM), vmem, vmem],
        out_specs=[vmem, vmem],
        out_shape=[
            jax.ShapeDtypeStruct((4, 4, 128, 256), BF16),
            jax.ShapeDtypeStruct((4, 3, 128, 256), BF16),
        ],
        scratch_shapes=[pltpu.VMEM((3, 64, 256), F32)],
        name="phases",
    )(source_position, momenta, jnp.asarray(site_places()))


def body(propagator, backward, sink_time, source_position, momenta, gamma_table):
    prop = propagator.reshape(288, ROWS, 1, 128)
    back = backward.reshape(288, ROWS, 1, 128)
    upper = [None, *source([(1, 0), (2, 0), (3, 0)], sink_time, prop)]
    lower = [None, *source([(1, 1), (2, 1), (3, 1)], sink_time, prop)]
    upper[0], lower[0] = source([(0, 0), (0, 1)], sink_time, prop)
    phases = phase_blocks(source_position, momenta)
    upper, lower, phases = spread(upper, lower, sink_time[0], phases)
    args = (sink_time, prop, back, phases)
    (sums,) = contract([(0, 0), (0, 1)], *args, [upper[0], lower[0]])
    (sums,) = contract([(k, 1) for k in (1, 2, 3)], *args, lower[1:], sums)
    keep, send = contract(
        [(k, 0) for k in (1, 2, 3)], *args, upper[1:], sums, jnp.asarray(gamma_weights()), gamma_table
    )
    return (keep + lax.ppermute(send, "gz", [(0, 1), (1, 0)]))[:, None]


def solution(mesh):
    in_specs = (
        P(None, None, None, "ta", "gz"),
        P(None, None, None, "ta", "gz"),
        P(),
        P(),
        P(),
        P(),
    )
    out_specs = P(None, "ta", "gz", None)
    return jax.shard_map(body, mesh=mesh, in_specs=in_specs, out_specs=out_specs, check_vma=False)
```

profile of v0, /device:TPU:1, one launch (start us, length us, event | category | flops | bytes accessed | tf_op | source)
XLA Modules:
  0.0 122.3 jit_solution(17210741350361157000)
XLA Ops:
  0.8 3.6 %collective-permute-start.3 = (f32[4,240,128]{2,1,0:T(8,128)}, f32[4,240,128]{2,1,0:T(8,128)S(1)}, u32[]{:S(2)}, u32[]{:S(2)}) collective-permute-start(f32[4,240,128]{2,1,0:T(8,128)} %get-tuple-element.30), channel_id=1, source_target_pairs={{0,8},{1,97},{2,10},{3,99},{4,12},{5,101},{6,14},{7,103},{8,16},{9... | collective-permute-start | bytes 1474568 | tf_op jit(solution)/shard_map/ppermute | solution.py:153
  4.4 3.8 %collective-permute-start.4 = (f32[4,240,128]{2,1,0:T(8,128)}, f32[4,240,128]{2,1,0:T(8,128)S(1)}, u32[]{:S(2)}, u32[]{:S(2)}) collective-permute-start(f32[4,240,128]{2,1,0:T(8,128)} %get-tuple-element.31), channel_id=1, source_target_pairs={{0,32},{1,7},{2,34},{3,1},{4,36},{5,3},{6,38},{7,5},{8,40},{9,15},... | collective-permute-start | bytes 1474568 | tf_op jit(solution)/shard_map/ppermute | solution.py:153
  8.2 2.5 %collective-permute-start.5 = (f32[4,240,128]{2,1,0:T(8,128)}, f32[4,240,128]{2,1,0:T(8,128)}, u32[]{:S(2)}, u32[]{:S(2)}) collective-permute-start(f32[4,240,128]{2,1,0:T(8,128)} %get-tuple-element.32), channel_id=1, source_target_pairs={{0,2},{1,25},{2,4},{3,27},{4,6},{5,29},{6,0},{7,31},{8,10},{9,1},{... | collective-permute-start | bytes 1474568 | tf_op jit(solution)/shard_map/ppermute | solution.py:153
  10.8 2.7 %collective-permute-start = (f32[4,320,128]{2,1,0:T(8,128)}, f32[4,320,128]{2,1,0:T(8,128)S(1)}, u32[]{:S(2)}, u32[]{:S(2)}) collective-permute-start(f32[4,320,128]{2,1,0:T(8,128)} %get-tuple-element.26), channel_id=1, source_target_pairs={{0,8},{1,97},{2,10},{3,99},{4,12},{5,101},{6,14},{7,103},{8,16},{9... | collective-permute-start | bytes 1966088 | tf_op jit(solution)/shard_map/ppermute | solution.py:153
  14.2 4.4 %phases.1 = (bf16[4,4,128,256]{3,2,1,0:T(8,128)(2,1)}, bf16[4,3,128,256]{3,2,1,0:T(8,128)(2,1)}) custom-call(s32[3]{0:T(128)} %source_ref.1, s32[27,3]{1,0:T(8,128)} %copy.9.momenta, f32[28,8,256]{2,1,0:T(8,128)} %constant.30.clone.places), custom_call_target="tpu_custom_call" | custom-call | tf_op jit(solution)/shard_map/phases/pallas_call | solution.py:459
  21.3 2.1 %collective-permute-done.1 = f32[4,320,128]{2,1,0:T(8,128)S(1)} collective-permute-done((f32[4,320,128]{2,1,0:T(8,128)}, f32[4,320,128]{2,1,0:T(8,128)S(1)}, u32[]{:S(2)}, u32[]{:S(2)}) %collective-permute-start.1) | collective-permute-done | bytes 655392 | tf_op jit(solution)/shard_map/ppermute | solution.py:153
  25.1 2.4 %collective-permute-start.8 = (f32[560,128]{1,0:T(8,128)S(1)}, f32[560,128]{1,0:T(8,128)S(1)}, u32[]{:S(2)}, u32[]{:S(2)}) collective-permute-start(f32[560,128]{1,0:T(8,128)S(1)} %pad_maximum_fusion.4), channel_id=1, source_target_pairs={{0,4},{1,17},{2,6},{3,19},{4,0},{5,21},{6,2},{7,23},{8,12},{9,25},... | collective-permute-start | bytes 860168 | tf_op jit(solution)/shard_map/ppermute | solution.py:153
  28.3 2.5 %collective-permute-start.6 = (f32[560,128]{1,0:T(8,128)S(1)}, f32[560,128]{1,0:T(8,128)S(1)}, u32[]{:S(2)}, u32[]{:S(2)}) collective-permute-start(f32[560,128]{1,0:T(8,128)S(1)} %pad_maximum_fusion.2), channel_id=1, source_target_pairs={{0,16},{1,65},{2,18},{3,67},{4,20},{5,69},{6,22},{7,71},{8,24},{9,... | collective-permute-start | bytes 860168 | tf_op jit(solution)/shard_map/ppermute | solution.py:153
  30.8 1.7 %collective-permute-done.8 = f32[560,128]{1,0:T(8,128)S(1)} collective-permute-done((f32[560,128]{1,0:T(8,128)S(1)}, f32[560,128]{1,0:T(8,128)S(1)}, u32[]{:S(2)}, u32[]{:S(2)}) %collective-permute-start.8) | collective-permute-done | bytes 286752 | tf_op jit(solution)/shard_map/ppermute | solution.py:153
  32.5 5.2 %collective-permute-done.7 = f32[560,128]{1,0:T(8,128)S(1)} collective-permute-done((f32[560,128]{1,0:T(8,128)S(1)}, f32[560,128]{1,0:T(8,128)S(1)}, u32[]{:S(2)}, u32[]{:S(2)}) %collective-permute-start.7) | collective-permute-done | bytes 286752 | tf_op jit(solution)/shard_map/ppermute | solution.py:153
  37.7 7.2 %collective-permute-start.10 = (f32[560,128]{1,0:T(8,128)S(1)}, f32[560,128]{1,0:T(8,128)S(1)}, u32[]{:S(2)}, u32[]{:S(2)}) collective-permute-start(f32[560,128]{1,0:T(8,128)S(1)} %maximum_select_fusion), channel_id=1, source_target_pairs={{0,84},{1,85},{2,86},{3,87},{4,80},{5,81},{6,82},{7,83},{8,92},{9,... | collective-permute-start | bytes 860168 | tf_op jit(solution)/shard_map/ppermute | solution.py:153
  44.9 6.9 %collective-permute-start.9 = (f32[560,128]{1,0:T(8,128)S(1)}, f32[560,128]{1,0:T(8,128)S(1)}, u32[]{:S(2)}, u32[]{:S(2)}) collective-permute-start(f32[560,128]{1,0:T(8,128)S(1)} %maximum_select_fusion), channel_id=1, source_target_pairs={{0,42},{1,127},{2,44},{3,121},{4,46},{5,123},{6,40},{7,125},{8,50}... | collective-permute-start | bytes 860168 | tf_op jit(solution)/shard_map/ppermute | solution.py:153
  51.8 10.9 %collective-permute-done.11 = f32[560,128]{1,0:T(8,128)S(1)} collective-permute-done((f32[560,128]{1,0:T(8,128)S(1)}, f32[560,128]{1,0:T(8,128)S(1)}, u32[]{:S(2)}, u32[]{:S(2)}) %collective-permute-start.11) | collective-permute-done | bytes 286752 | tf_op jit(solution)/shard_map/ppermute | solution.py:153
  63.8 2.6 %collective-permute-start.12 = (f32[560,128]{1,0:T(8,128)S(1)}, f32[560,128]{1,0:T(8,128)S(1)}, u32[]{:S(2)}, u32[]{:S(2)}) collective-permute-start(f32[560,128]{1,0:T(8,128)S(1)} %select_select_fusion), channel_id=1, source_target_pairs={{0,16},{1,65},{2,18},{3,67},{4,20},{5,69},{6,22},{7,71},{8,24},{9,... | collective-permute-start | bytes 860168 | tf_op jit(solution)/shard_map/ppermute | solution.py:153
  66.5 3.7 %collective-permute-done.14 = f32[560,128]{1,0:T(8,128)S(1)} collective-permute-done((f32[560,128]{1,0:T(8,128)S(1)}, f32[560,128]{1,0:T(8,128)S(1)}, u32[]{:S(2)}, u32[]{:S(2)}) %collective-permute-start.14) | collective-permute-done | bytes 286752 | tf_op jit(solution)/shard_map/ppermute | solution.py:153
  70.7 2.1 %collective-permute-done.12 = f32[560,128]{1,0:T(8,128)S(1)} collective-permute-done((f32[560,128]{1,0:T(8,128)S(1)}, f32[560,128]{1,0:T(8,128)S(1)}, u32[]{:S(2)}, u32[]{:S(2)}) %collective-permute-start.12) | collective-permute-done | bytes 286752 | tf_op jit(solution)/shard_map/ppermute | solution.py:153
  72.9 3.9 %collective-permute-start.18 = (f32[4,240,128]{2,1,0:T(8,128)S(1)}, f32[4,240,128]{2,1,0:T(8,128)S(1)}, u32[]{:S(2)}, u32[]{:S(2)}) collective-permute-start(f32[4,240,128]{2,1,0:T(8,128)S(1)} %pad_maximum_fusion.1.refs_6_), channel_id=1, source_target_pairs={{0,8},{1,97},{2,10},{3,99},{4,12},{5,101},{6,14},{7,103},{8,16},{9... | collective-permute-start | bytes 1474568 | tf_op jit(solution)/shard_map/ppermute | solution.py:153
  77.0 1.4 %collective-permute-start.16 = (f32[4,320,128]{2,1,0:T(8,128)S(1)}, f32[4,320,128]{2,1,0:T(8,128)S(1)}, u32[]{:S(2)}, u32[]{:S(2)}) collective-permute-start(f32[4,320,128]{2,1,0:T(8,128)S(1)} %pad_maximum_fusion.refs_5_), channel_id=1, source_target_pairs={{0,32},{1,7},{2,34},{3,1},{4,36},{5,3},{6,38},{7,5},{8,40},{9,15},... | collective-permute-start | bytes 1966088 | tf_op jit(solution)/shard_map/ppermute | solution.py:153
  79.6 1.4 %collective-permute-start.19 = (f32[4,240,128]{2,1,0:T(8,128)S(1)}, f32[4,240,128]{2,1,0:T(8,128)}, u32[]{:S(2)}, u32[]{:S(2)}) collective-permute-start(f32[4,240,128]{2,1,0:T(8,128)S(1)} %pad_maximum_fusion.1.refs_6_), channel_id=1, source_target_pairs={{0,32},{1,7},{2,34},{3,1},{4,36},{5,3},{6,38},{7,5},{8,40},{9,15},... | collective-permute-start | bytes 1474568 | tf_op jit(solution)/shard_map/ppermute | solution.py:153
  81.0 1.6 %collective-permute-done.18.refs_5_ = f32[4,240,128]{2,1,0:T(8,128)S(1)} collective-permute-done((f32[4,240,128]{2,1,0:T(8,128)S(1)}, f32[4,240,128]{2,1,0:T(8,128)S(1)}, u32[]{:S(2)}, u32[]{:S(2)}) %collective-permute-start.18) | collective-permute-done | bytes 491552 | tf_op jit(solution)/shard_map/ppermute | solution.py:153
  84.7 7.4 %shard_map.85.refs_8_ = f32[64,128]{1,0:T(8,128)} custom-call(s32[1]{0:T(128)S(6)} %copy.11.refs_0_, f32[288,54,1,128]{3,2,1,0:T(1,128)} %bitcast.44, f32[288,54,1,128]{3,2,1,0:T(1,128)} %bitcast.47, bf16[4,4,128,256]{3,2,1,0:T(8,128)(2,1)} %get-tuple-element.22.refs_3_, bf16[4,3,128,256]{3,2,1,0:T(8,128)(2,1)} %get-tuple-element.23.refs_4_, ...), custom_call_target="tpu_custom_call" | custom-call | tf_op jit(solution)/shard_map/pallas_call | solution.py:376
  93.5 10.7 %shard_map.86.refs_8_ = f32[64,128]{1,0:T(8,128)} custom-call(s32[1]{0:T(128)S(6)} %copy.11.refs_0_, f32[288,54,1,128]{3,2,1,0:T(1,128)} %bitcast.45, f32[288,54,1,128]{3,2,1,0:T(1,128)} %bitcast.48, bf16[4,4,128,256]{3,2,1,0:T(8,128)(2,1)} %get-tuple-element.22.refs_3_, bf16[4,3,128,256]{3,2,1,0:T(8,128)(2,1)} %get-tuple-element.23.refs_4_, ...), custom_call_target="tpu_custom_call" | custom-call | tf_op jit(solution)/shard_map/pallas_call | solution.py:376
  106.2 11.3 %shard_map.87 = (f32[2,8,27]{2,1,0:T(8,128)}, f32[2,8,27]{2,1,0:T(8,128)}) custom-call(s32[1]{0:T(128)S(6)} %copy.11.refs_0_, f32[288,54,1,128]{3,2,1,0:T(1,128)} %bitcast.46, f32[288,54,1,128]{3,2,1,0:T(1,128)} %bitcast.49, bf16[4,4,128,256]{3,2,1,0:T(8,128)(2,1)} %get-tuple-element.22.refs_3_, bf16[4,3,128,256]{3,2,1,0:T(8,128)(2,1)} %get-tuple-element.23.refs_4_, ...), custom_call_target="tpu_custom_call" | custom-call | tf_op jit(solution)/shard_map/pallas_call | solution.py:376
  117.5 2.5 %collective-permute-start.21 = (f32[2,8,27]{2,1,0:T(8,128)}, f32[2,8,27]{2,1,0:T(8,128)S(1)}, u32[]{:S(2)}, u32[]{:S(2)}) collective-permute-start(f32[2,8,27]{2,1,0:T(8,128)} %get-tuple-element.34), channel_id=1, source_target_pairs={{0,1},{1,0},{2,3},{3,2},{4,5},{5,4},{6,7},{7,6},{8,9},{9,8},{10,11... | collective-permute-start | bytes 5192 | tf_op jit(solution)/shard_map/ppermute | solution.py:486
  (60 shorter events, 17.0 us)
Async XLA Ops:
  0.7 12.9 %copy-start.6 = (s32[27,3]{0,1:T(4,128)S(1)}, s32[27,3]{0,1:T(4,128)}, u32[]{:S(2)}) copy-start(s32[27,3]{0,1:T(4,128)} %param.12) | copy-start | bytes 976
  0.8 12.7 %collective-permute-start.3 = (f32[4,240,128]{2,1,0:T(8,128)}, f32[4,240,128]{2,1,0:T(8,128)S(1)}, u32[]{:S(2)}, u32[]{:S(2)}) collective-permute-start(f32[4,240,128]{2,1,0:T(8,128)} %get-tuple-element.30), channel_id=1, source_target_pairs={{0,8},{1,97},{2,10},{3,99},{4,12},{5,101},{6,14},{7,103},{8,16},{9... | collective-permute-start | bytes 1474568 | tf_op jit(solution)/shard_map/ppermute | solution.py:153
  4.4 14.4 %collective-permute-start.4 = (f32[4,240,128]{2,1,0:T(8,128)}, f32[4,240,128]{2,1,0:T(8,128)S(1)}, u32[]{:S(2)}, u32[]{:S(2)}) collective-permute-start(f32[4,240,128]{2,1,0:T(8,128)} %get-tuple-element.31), channel_id=1, source_target_pairs={{0,32},{1,7},{2,34},{3,1},{4,36},{5,3},{6,38},{7,5},{8,40},{9,15},... | collective-permute-start | bytes 1474568 | tf_op jit(solution)/shard_map/ppermute | solution.py:153
  8.2 10.6 %collective-permute-start.5 = (f32[4,240,128]{2,1,0:T(8,128)}, f32[4,240,128]{2,1,0:T(8,128)}, u32[]{:S(2)}, u32[]{:S(2)}) collective-permute-start(f32[4,240,128]{2,1,0:T(8,128)} %get-tuple-element.32), channel_id=1, source_target_pairs={{0,2},{1,25},{2,4},{3,27},{4,6},{5,29},{6,0},{7,31},{8,10},{9,1},{... | collective-permute-start | bytes 1474568 | tf_op jit(solution)/shard_map/ppermute | solution.py:153
  10.8 10.5 %collective-permute-start = (f32[4,320,128]{2,1,0:T(8,128)}, f32[4,320,128]{2,1,0:T(8,128)S(1)}, u32[]{:S(2)}, u32[]{:S(2)}) collective-permute-start(f32[4,320,128]{2,1,0:T(8,128)} %get-tuple-element.26), channel_id=1, source_target_pairs={{0,8},{1,97},{2,10},{3,99},{4,12},{5,101},{6,14},{7,103},{8,16},{9... | collective-permute-start | bytes 1966088 | tf_op jit(solution)/shard_map/ppermute | solution.py:153
  13.5 9.9 %collective-permute-start.1 = (f32[4,320,128]{2,1,0:T(8,128)}, f32[4,320,128]{2,1,0:T(8,128)S(1)}, u32[]{:S(2)}, u32[]{:S(2)}) collective-permute-start(f32[4,320,128]{2,1,0:T(8,128)} %get-tuple-element.27), channel_id=1, source_target_pairs={{0,32},{1,7},{2,34},{3,1},{4,36},{5,3},{6,38},{7,5},{8,40},{9,15},... | collective-permute-start | bytes 1966088 | tf_op jit(solution)/shard_map/ppermute | solution.py:153
  13.5 10.3 %collective-permute-start.2 = (f32[4,320,128]{2,1,0:T(8,128)}, f32[4,320,128]{2,1,0:T(8,128)S(1)}, u32[]{:S(2)}, u32[]{:S(2)}) collective-permute-start(f32[4,320,128]{2,1,0:T(8,128)} %get-tuple-element.28), channel_id=1, source_target_pairs={{0,2},{1,25},{2,4},{3,27},{4,6},{5,29},{6,0},{7,31},{8,10},{9,1},{... | collective-permute-start | bytes 1966088 | tf_op jit(solution)/shard_map/ppermute | solution.py:153
  25.1 7.4 %collective-permute-start.8 = (f32[560,128]{1,0:T(8,128)S(1)}, f32[560,128]{1,0:T(8,128)S(1)}, u32[]{:S(2)}, u32[]{:S(2)}) collective-permute-start(f32[560,128]{1,0:T(8,128)S(1)} %pad_maximum_fusion.4), channel_id=1, source_target_pairs={{0,4},{1,17},{2,6},{3,19},{4,0},{5,21},{6,2},{7,23},{8,12},{9,25},... | collective-permute-start | bytes 860168 | tf_op jit(solution)/shard_map/ppermute | solution.py:153
  27.6 10.1 %collective-permute-start.7 = (f32[560,128]{1,0:T(8,128)S(1)}, f32[560,128]{1,0:T(8,128)S(1)}, u32[]{:S(2)}, u32[]{:S(2)}) collective-permute-start(f32[560,128]{1,0:T(8,128)S(1)} %pad_maximum_fusion.3), channel_id=1, source_target_pairs={{0,64},{1,5},{2,66},{3,7},{4,68},{5,1},{6,70},{7,3},{8,72},{9,13},... | collective-permute-start | bytes 860168 | tf_op jit(solution)/shard_map/ppermute | solution.py:153
  28.3 9.3 %collective-permute-start.6 = (f32[560,128]{1,0:T(8,128)S(1)}, f32[560,128]{1,0:T(8,128)S(1)}, u32[]{:S(2)}, u32[]{:S(2)}) collective-permute-start(f32[560,128]{1,0:T(8,128)S(1)} %pad_maximum_fusion.2), channel_id=1, source_target_pairs={{0,16},{1,65},{2,18},{3,67},{4,20},{5,69},{6,22},{7,71},{8,24},{9,... | collective-permute-start | bytes 860168 | tf_op jit(solution)/shard_map/ppermute | solution.py:153
  37.7 14.1 %collective-permute-start.10 = (f32[560,128]{1,0:T(8,128)S(1)}, f32[560,128]{1,0:T(8,128)S(1)}, u32[]{:S(2)}, u32[]{:S(2)}) collective-permute-start(f32[560,128]{1,0:T(8,128)S(1)} %maximum_select_fusion), channel_id=1, source_target_pairs={{0,84},{1,85},{2,86},{3,87},{4,80},{5,81},{6,82},{7,83},{8,92},{9,... | collective-permute-start | bytes 860168 | tf_op jit(solution)/shard_map/ppermute | solution.py:153
  44.9 17.8 %collective-permute-start.11 = (f32[560,128]{1,0:T(8,128)S(1)}, f32[560,128]{1,0:T(8,128)S(1)}, u32[]{:S(2)}, u32[]{:S(2)}) collective-permute-start(f32[560,128]{1,0:T(8,128)S(1)} %maximum_select_fusion), channel_id=1, source_target_pairs={{0,126},{1,43},{2,120},{3,45},{4,122},{5,47},{6,124},{7,41},{8,102... | collective-permute-start | bytes 860168 | tf_op jit(solution)/shard_map/ppermute | solution.py:153
  44.9 17.8 %collective-permute-start.9 = (f32[560,128]{1,0:T(8,128)S(1)}, f32[560,128]{1,0:T(8,128)S(1)}, u32[]{:S(2)}, u32[]{:S(2)}) collective-permute-start(f32[560,128]{1,0:T(8,128)S(1)} %maximum_select_fusion), channel_id=1, source_target_pairs={{0,42},{1,127},{2,44},{3,121},{4,46},{5,123},{6,40},{7,125},{8,50}... | collective-permute-start | bytes 860168 | tf_op jit(solution)/shard_map/ppermute | solution.py:153
  62.8 7.4 %collective-permute-start.14 = (f32[560,128]{1,0:T(8,128)S(1)}, f32[560,128]{1,0:T(8,128)S(1)}, u32[]{:S(2)}, u32[]{:S(2)}) collective-permute-start(f32[560,128]{1,0:T(8,128)S(1)} %select_select_fusion), channel_id=1, source_target_pairs={{0,4},{1,17},{2,6},{3,19},{4,0},{5,21},{6,2},{7,23},{8,12},{9,25},... | collective-permute-start | bytes 860168 | tf_op jit(solution)/shard_map/ppermute | solution.py:153
  62.9 7.9 %collective-permute-start.13 = (f32[560,128]{1,0:T(8,128)S(1)}, f32[560,128]{1,0:T(8,128)S(1)}, u32[]{:S(2)}, u32[]{:S(2)}) collective-permute-start(f32[560,128]{1,0:T(8,128)S(1)} %select_select_fusion), channel_id=1, source_target_pairs={{0,64},{1,5},{2,66},{3,7},{4,68},{5,1},{6,70},{7,3},{8,72},{9,13},... | collective-permute-start | bytes 860168 | tf_op jit(solution)/shard_map/ppermute | solution.py:153
  63.8 9.0 %collective-permute-start.12 = (f32[560,128]{1,0:T(8,128)S(1)}, f32[560,128]{1,0:T(8,128)S(1)}, u32[]{:S(2)}, u32[]{:S(2)}) collective-permute-start(f32[560,128]{1,0:T(8,128)S(1)} %select_select_fusion), channel_id=1, source_target_pairs={{0,16},{1,65},{2,18},{3,67},{4,20},{5,69},{6,22},{7,71},{8,24},{9,... | collective-permute-start | bytes 860168 | tf_op jit(solution)/shard_map/ppermute | solution.py:153
  72.9 11.8 %copy-start.1 = (f32[4,240,128]{2,1,0:T(8,128)}, f32[4,240,128]{2,1,0:T(8,128)S(1)}, u32[]{:S(2)}) copy-start(f32[4,240,128]{2,1,0:T(8,128)S(1)} %pad_maximum_fusion.1.refs_6_) | copy-start | bytes 1474564
  72.9 9.7 %collective-permute-start.18 = (f32[4,240,128]{2,1,0:T(8,128)S(1)}, f32[4,240,128]{2,1,0:T(8,128)S(1)}, u32[]{:S(2)}, u32[]{:S(2)}) collective-permute-start(f32[4,240,128]{2,1,0:T(8,128)S(1)} %pad_maximum_fusion.1.refs_6_), channel_id=1, source_target_pairs={{0,8},{1,97},{2,10},{3,99},{4,12},{5,101},{6,14},{7,103},{8,16},{9... | collective-permute-start | bytes 1474568 | tf_op jit(solution)/shard_map/ppermute | solution.py:153
  76.9 27.3 %collective-permute-start.15 = (f32[4,320,128]{2,1,0:T(8,128)S(1)}, f32[4,320,128]{2,1,0:T(8,128)S(1)}, u32[]{:S(2)}, u32[]{:S(2)}) collective-permute-start(f32[4,320,128]{2,1,0:T(8,128)S(1)} %pad_maximum_fusion.refs_5_), channel_id=1, source_target_pairs={{0,8},{1,97},{2,10},{3,99},{4,12},{5,101},{6,14},{7,103},{8,16},{9... | collective-permute-start | bytes 1966088 | tf_op jit(solution)/shard_map/ppermute | solution.py:153
  77.0 27.2 %collective-permute-start.16 = (f32[4,320,128]{2,1,0:T(8,128)S(1)}, f32[4,320,128]{2,1,0:T(8,128)S(1)}, u32[]{:S(2)}, u32[]{:S(2)}) collective-permute-start(f32[4,320,128]{2,1,0:T(8,128)S(1)} %pad_maximum_fusion.refs_5_), channel_id=1, source_target_pairs={{0,32},{1,7},{2,34},{3,1},{4,36},{5,3},{6,38},{7,5},{8,40},{9,15},... | collective-permute-start | bytes 1966088 | tf_op jit(solution)/shard_map/ppermute | solution.py:153
  78.4 25.8 %collective-permute-start.17 = (f32[4,320,128]{2,1,0:T(8,128)S(1)}, f32[4,320,128]{2,1,0:T(8,128)S(1)}, u32[]{:S(2)}, u32[]{:S(2)}) collective-permute-start(f32[4,320,128]{2,1,0:T(8,128)S(1)} %pad_maximum_fusion.refs_5_), channel_id=1, source_target_pairs={{0,2},{1,25},{2,4},{3,27},{4,6},{5,29},{6,0},{7,31},{8,10},{9,1},{... | collective-permute-start | bytes 1966088 | tf_op jit(solution)/shard_map/ppermute | solution.py:153
  79.6 12.6 %collective-permute-start.19 = (f32[4,240,128]{2,1,0:T(8,128)S(1)}, f32[4,240,128]{2,1,0:T(8,128)}, u32[]{:S(2)}, u32[]{:S(2)}) collective-permute-start(f32[4,240,128]{2,1,0:T(8,128)S(1)} %pad_maximum_fusion.1.refs_6_), channel_id=1, source_target_pairs={{0,32},{1,7},{2,34},{3,1},{4,36},{5,3},{6,38},{7,5},{8,40},{9,15},... | collective-permute-start | bytes 1474568 | tf_op jit(solution)/shard_map/ppermute | solution.py:153
  83.4 10.2 %collective-permute-start.20 = (f32[4,240,128]{2,1,0:T(8,128)S(1)}, f32[4,240,128]{2,1,0:T(8,128)}, u32[]{:S(2)}, u32[]{:S(2)}) collective-permute-start(f32[4,240,128]{2,1,0:T(8,128)S(1)} %pad_maximum_fusion.1.refs_6_), channel_id=1, source_target_pairs={{0,2},{1,25},{2,4},{3,27},{4,6},{5,29},{6,0},{7,31},{8,10},{9,1},{... | collective-permute-start | bytes 1474568 | tf_op jit(solution)/shard_map/ppermute | solution.py:153
  117.5 3.6 %collective-permute-start.21 = (f32[2,8,27]{2,1,0:T(8,128)}, f32[2,8,27]{2,1,0:T(8,128)S(1)}, u32[]{:S(2)}, u32[]{:S(2)}) collective-permute-start(f32[2,8,27]{2,1,0:T(8,128)} %get-tuple-element.34), channel_id=1, source_target_pairs={{0,1},{1,0},{2,3},{3,2},{4,5},{5,4},{6,7},{7,6},{8,9},{9,8},{10,11... | collective-permute-start | bytes 5192 | tf_op jit(solution)/shard_map/ppermute | solution.py:486
  (5 other events, 11.3 us)
where the time goes:
time: 123 us; the launch traced here: 122 us
  starting transfers between devices  47.7 us (39%)
  Pallas kernels  34.2 us (28%)
  waiting for transfers between devices  31.8 us (26%)
  other arithmetic  4.24 us (3%)
  local copies, waits for them, and re-layouts  3.45 us (3%)
    ppermute x21, starting transfers between devices, shift(): return lax.ppermute(value, ('ta', 'gz'), moved(vector))  45.2 us
    ppermute x21, waiting for transfers between devices, shift(): return lax.ppermute(value, ('ta', 'gz'), moved(vector))  30.8 us
    pallas_call x3, Pallas kernels, contract(): pl.pallas_call(kernel, in_specs=[smem] + [anywhere] * (4 + nb) + [vmem] *...  29.4 us
    pallas_call x1, Pallas kernels, phase_blocks(): pl.pallas_call(phase_kernel, in_specs=[pl.BlockSpec(memory_space=pltpu.SM...  4.45 us
    unnamed x15, local copies, waits for them, and re-layouts  3.37 us
    select_n x4, other arithmetic, pick(): value = jnp.where(index == i, sources[i], value)  2.8 us
    ppermute x1, starting transfers between devices, body(): return (keep + lax.ppermute(send, 'gz', [(0, 1), (1, 0)]))[:, None]  2.53 us
  transfers between devices with their start and end apart: 22, of which 13 were waited for; matrix products, arithmetic and copies ran while one was open for 2% of the time, Pallas kernels for 19%

commit v1 on v0

--- a/solution.py
+++ b/solution.py
@@ -37,19 +37,10 @@
     return np.concatenate([top, low]).astype(np.float32)
 
 
-PIECES = 4
-
-
-def block_copies(field, start, rows, buf, sems):
-    span = 288 // PIECES
-    return [
-        pltpu.make_async_copy(
-            field.at[pl.ds(i * span, span), pl.ds(start, rows), 0, :],
-            buf.at[pl.ds(i * span, span), pl.ds(0, rows), :],
-            sems.at[i],
-        )
-        for i in range(PIECES)
-    ]
+def block_copy(field, start, rows, buf, row, sem):
+    return pltpu.make_async_copy(
+        field.at[:, pl.ds(start, rows), 0, :], buf.at[:, pl.ds(row, rows), :], sem
+    )
 
 
 def source_block(buf, sums, write):
@@ -78,24 +69,21 @@
 
     @pl.when(lax.axis_index("ta") == sink_ref[0])
     def _():
-        def copies_in(i):
+        def copy_in(i):
             quarter, half = blocks[i]
             start = (A_START, B_START)[half][quarter]
-            return block_copies(field, start, 8 - 2 * half, bufs.at[i], sems.at[i])
+            return block_copy(field, start, 8 - 2 * half, bufs.at[i], 0, sems.at[i])
 
         def copy_out(i):
             rows = 40 * (8 - 2 * blocks[i][1])
             return pltpu.make_async_copy(stage.at[i, :, pl.ds(0, rows), :], outs[i], out_sems.at[i])
 
         for i in range(min(2, len(blocks))):
-            for copy in copies_in(i):
-                copy.start()
+            copy_in(i).start()
         for i, (_, half) in enumerate(blocks):
-            for copy in copies_in(i):
-                copy.wait()
+            copy_in(i).wait()
             if i + 2 < len(blocks):
-                for copy in copies_in(i + 2):
-                    copy.start()
+                copy_in(i + 2).start()
 
             def write(u, re, im, i=i, rows=8 - 2 * half):
                 for e, v in ((u, re), (78 + u, im)):
@@ -124,7 +112,7 @@
             pltpu.VMEM((count, 288, 8, 128), F32),
             pltpu.VMEM((count, 4, 320, 128), F32),
             pltpu.VMEM((144, 8, 128), F32),
-            pltpu.SemaphoreType.DMA((count, PIECES)),
+            pltpu.SemaphoreType.DMA((count,)),
             pltpu.SemaphoreType.DMA((count,)),
         ],
     )(sink_time, field)
@@ -210,14 +198,19 @@
     return [upper] + upper_got, [lower] + lower_got, ready
 
 
-def contract_block(rows, b, slots, s_buf, h_buf, g_buf, sig, s_sum, h_sum, macc, mout):
+def unpack(b, parts, slots, g_buf, sig):
     for u in range(78):
-        part = []
-        for e in (u, 78 + u):
-            v = g_buf[b, slots[e // 39], e % 39 * rows : e % 39 * rows + rows, :]
-            sig[(e // 78) * 78 + u, 0:rows, :] = v
-            part.append(v)
-        sig[156 + u, 0:rows, :] = part[0] + part[1]
+        for f, row, skip, count, rows in parts:
+            both = []
+            for e in (u, 78 + u):
+                first = e % 39 * rows + skip
+                v = g_buf[f, slots[f][e // 39], first : first + count, :]
+                sig[b, e, row : row + count, :] = v
+                both.append(v)
+            sig[b, 156 + u, row : row + count, :] = both[0] + both[1]
+
+
+def contract_block(b, s_buf, h_buf, sig, s_sum, h_sum, macc, mout):
     for e in range(144):
         s_sum[e] = s_buf[b, e] + s_buf[b, 144 + e]
         h_sum[e] = h_buf[b, e] + h_buf[b, 144 + e]
@@ -233,7 +226,7 @@
                 ]
                 for n in range(nt, nt + 3):
                     u = pair_index(m, n)
-                    g = (sig[u], sig[78 + u], sig[156 + u])
+                    g = (sig[b, u], sig[b, 78 + u], sig[b, 156 + u])
                     for a in range(3):
                         new = tuple(x * y for x, y in zip(h[a], g))
                         acc[a, n] = new if m == 0 else tuple(x + y for x, y in zip(acc[a, n], new))
@@ -261,8 +254,8 @@
     lax.fori_loop(0, 4, spin, 0)
 
 
-def project(rows, mout, phases, total):
-    for pair in range(rows // 2):
+def project(mout, phases, total):
+    for pair in range(4):
         wide = jnp.concatenate([mout[:, 2 * pair, :], mout[:, 2 * pair + 1, :]], axis=1)
         high = wide.astype(BF16)
         low = (wide - high.astype(F32)).astype(BF16)
@@ -290,9 +283,11 @@
     return tuple(result[8 * i : 8 * i + 8] for i in range(4))
 
 
-def contract_kernel(blocks, more, last, sink_ref, prop, back, phases_a, phases_b, *refs):
-    nb = len(blocks)
-    fields, refs = refs[:nb], refs[nb:]
+def contract_kernel(half, numbered, more, last, sink_ref, prop, back, phases, *refs):
+    rows = 8 - 2 * half
+    nf = len(numbered)
+    nb = nf * rows // 8
+    fields, refs = refs[:nf], refs[nf:]
     if more:
         before, refs = refs[0], refs[1:]
     if last:
@@ -300,53 +295,60 @@
         refs = refs[4:]
     else:
         out_ref, refs = refs[0], refs[1:]
-    s_buf, h_buf, g_buf, p_buf, sig, s_sum, h_sum, macc, mout, acc, numbers, sems = refs
+    s_buf, h_buf, g_buf, p_buf, sig, s_sum, h_sum, macc, mout, acc, numbers, sems, g_sems = refs
+    parts = []
+    for b in range(nb):
+        parts.append([])
+        row = 0
+        while row < 8:
+            f, skip = divmod(8 * b + row, rows)
+            count = min(rows - skip, 8 - row)
+            parts[b].append((f, row, skip, count, rows))
+            row += count
+    opens = [sorted({p[0] for p in parts[b]} - {p[0] for q in parts[:b] for p in q}) for b in range(nb)]
 
     def copies(b):
-        half = blocks[b][1]
-        rows = 8 - 2 * half
-        starts, phases = ((A_START, phases_a), (B_START, phases_b))[half]
-        start = jnp.int32(starts[3])
-        for i in range(3):
-            start = jnp.where(numbers[b, 0] == i, starts[i], start)
-        return [
-            pltpu.make_async_copy(
-                fields[b], g_buf.at[b, :, pl.ds(0, 40 * rows), :], sems.at[b, 2 * PIECES]
-            ),
-            *block_copies(back, start, rows, h_buf.at[b], sems.at[b, pl.ds(0, PIECES)]),
-            *block_copies(prop, start, rows, s_buf.at[b], sems.at[b, pl.ds(PIECES, PIECES)]),
-            pltpu.make_async_copy(
-                phases.at[numbers[b, 0]], p_buf.at[b, pl.ds(0, rows // 2)], sems.at[b, 2 * PIECES + 1]
-            ),
-        ]
-
-    def on(b, action):
+        out = [pltpu.make_async_copy(fields[f], g_buf.at[f], g_sems.at[f]) for f in opens[b]]
+        for i, (f, row, skip, count, _) in enumerate(parts[b]):
+            starts = (A_START, B_START)[half]
+            start = jnp.int32(starts[3])
+            for q in range(3):
+                start = jnp.where(numbers[f, 0] == q, starts[q], start)
+            out += [
+                block_copy(back, start + skip, count, h_buf.at[b], row, sems.at[b, i, 0]),
+                block_copy(prop, start + skip, count, s_buf.at[b], row, sems.at[b, i, 1]),
+                pltpu.make_async_copy(
+                    phases.at[numbers[f, 0], pl.ds(skip // 2, count // 2)],
+                    p_buf.at[b, pl.ds(row // 2, count // 2)],
+                    sems.at[b, i, 2],
+                ),
+            ]
+        return out
+
+    for f, k in enumerate(numbered):
+        numbers[f, 0], numbers[f, 1] = received(sink_ref[0], k)
+    for copy in copies(0):
+        copy.start()
+    acc[...] = before[...] if more else jnp.zeros_like(acc)
+
+    def block(b, carry):
         for i in range(nb):
 
             @pl.when(b == i)
             def _():
                 for copy in copies(i):
-                    action(copy)
-
-    for b, (k, _) in enumerate(blocks):
-        numbers[b, 0], numbers[b, 1] = received(sink_ref[0], k)
-    for copy in copies(0):
-        copy.start()
-    acc[...] = before[...] if more else jnp.zeros_like(acc)
-    for half in (0, 1):
-        chosen = [b for b in range(nb) if blocks[b][1] == half]
-        rows = 8 - 2 * half
-
-        def block(b, carry, rows=rows):
-            on(b, lambda copy: copy.wait())
-            on(b + 1, lambda copy: copy.start())
-            slots = [numbers[b, 1] ^ g for g in range(4)]
-            contract_block(rows, b, slots, s_buf, h_buf, g_buf, sig, s_sum, h_sum, macc, mout)
-            acc[...] = project(rows, mout, p_buf.at[b], acc[...])
-            return carry
-
-        if chosen:
-            lax.fori_loop(chosen[0], chosen[-1] + 1, block, 0)
+                    copy.wait()
+                if i + 1 < nb:
+                    for copy in copies(i + 1):
+                        copy.start()
+                slots = {p[0]: [numbers[p[0], 1] ^ g for g in range(4)] for p in parts[i]}
+                unpack(i, parts[i], slots, g_buf, sig)
+
+        contract_block(b, s_buf, h_buf, sig, s_sum, h_sum, macc, mout)
+        acc[...] = project(mout, p_buf.at[b], acc[...])
+        return carry
+
+    lax.fori_loop(0, nb, block, 0)
     if last:
         mout[0, :, :28], mout[1, :, :28], mout[2, :, :28], mout[3, :, :28] = currents(weights[...], acc[...])
         core = lax.axis_index("gz")
@@ -359,12 +361,14 @@
         out_ref[...] = acc[...]
 
 
-def contract(blocks, sink_time, prop, back, phases, fields, before=None, weights=None, gammas=None):
-    nb = len(blocks)
+def contract(half, numbered, sink_time, prop, back, phases, fields, before=None, weights=None, gammas=None):
+    nf = len(numbered)
+    rows = 8 - 2 * half
+    nb = nf * rows // 8
     more, last = before is not None, weights is not None
 
     def kernel(*refs):
-        contract_kernel(blocks, more, last, *refs)
+        contract_kernel(half, numbered, more, last, *refs)
 
     anywhere = pl.BlockSpec(memory_space=pl.ANY)
     vmem = pl.BlockSpec(memory_space=pltpu.VMEM)
@@ -375,24 +379,25 @@
         out_shape = [jax.ShapeDtypeStruct((64, 128), F32)]
     return pl.pallas_call(
         kernel,
-        in_specs=[smem] + [anywhere] * (4 + nb) + [vmem] * more + [vmem, smem] * last,
+        in_specs=[smem] + [anywhere] * (3 + nf) + [vmem] * more + [vmem, smem] * last,
         out_specs=[vmem] * len(out_shape),
         out_shape=out_shape,
         scratch_shapes=[
             pltpu.VMEM((nb, 288, 8, 128), F32),
             pltpu.VMEM((nb, 288, 8, 128), F32),
-            pltpu.VMEM((nb, 4, 320, 128), F32),
+            pltpu.VMEM((nf, 4, 40 * rows, 128), F32),
             pltpu.VMEM((nb, 4, 128, 256), BF16),
-            pltpu.VMEM((234, 8, 128), F32),
+            pltpu.VMEM((nb, 234, 8, 128), F32),
             pltpu.VMEM((144, 8, 128), F32),
             pltpu.VMEM((144, 8, 128), F32),
             pltpu.VMEM((4, 3, 8, 128), F32),
             pltpu.VMEM((32, 8, 128), F32),
             pltpu.VMEM((64, 128), F32),
-            pltpu.SMEM((nb, 2), jnp.int32),
-            pltpu.SemaphoreType.DMA((nb, 2 * PIECES + 2)),
+            pltpu.SMEM((nf, 2), jnp.int32),
+            pltpu.SemaphoreType.DMA((nb, 2, 3)),
+            pltpu.SemaphoreType.DMA((nf,)),
         ],
-    )(sink_time, prop, back, *phases, *fields, *([before] if more else []), *([weights, gammas] if last else []))
+    )(sink_time, prop, back, phases, *fields, *([before] if more else []), *([weights, gammas] if last else []))
 
 
 def cosine_of(wave):
@@ -477,11 +482,10 @@
     upper[0], lower[0] = source([(0, 0), (0, 1)], sink_time, prop)
     phases = phase_blocks(source_position, momenta)
     upper, lower, phases = spread(upper, lower, sink_time[0], phases)
-    args = (sink_time, prop, back, phases)
-    (sums,) = contract([(0, 0), (0, 1)], *args, [upper[0], lower[0]])
-    (sums,) = contract([(k, 1) for k in (1, 2, 3)], *args, lower[1:], sums)
+    (sums,) = contract(0, (0,), sink_time, prop, back, phases[0], upper[:1])
+    (sums,) = contract(1, (0, 1, 2, 3), sink_time, prop, back, phases[1], lower, sums)
     keep, send = contract(
-        [(k, 0) for k in (1, 2, 3)], *args, upper[1:], sums, jnp.asarray(gamma_weights()), gamma_table
+        0, (1, 2, 3), sink_time, prop, back, phases[0], upper[1:], sums, jnp.asarray(gamma_weights()), gamma_table
     )
     return (keep + lax.ppermute(send, "gz", [(0, 1), (1, 0)]))[:, None]
 

time: 123 us -> 123 us (level)
  waiting for transfers between devices: 31.8 us -> 34.7 us
  Pallas kernels: 34.2 us -> 32 us
    ppermute x21, waiting for transfers between devices: 30.8 us -> 33.6 us  [shift(): return lax.ppermute(value, ('ta', 'gz'), moved(vector))]
    pallas_call x3, Pallas kernels: 29.4 us -> 27.4 us  [contract(): pl.pallas_call(kernel, in_specs=[smem] + [anywhere] * (3 + nf) + [vmem] *...]
  transfers between devices with their start and end apart: 22 -> 22, of which waited for: 13 -> 13; matrix products, arithmetic and copies ran while one was open for 2% -> 2% of each run, Pallas kernels for 19% -> 17%
where the time goes in v1:
time: 123 us
  starting transfers between devices  47.5 us (39%)
  waiting for transfers between devices  34.7 us (28%)
  Pallas kernels  32 us (26%)
  other arithmetic  4.24 us (3%)
  local copies, waits for them, and re-layouts  3.42 us (3%)
    ppermute x21, starting transfers between devices, shift(): return lax.ppermute(value, ('ta', 'gz'), moved(vector))  44.6 us
    ppermute x21, waiting for transfers between devices, shift(): return lax.ppermute(value, ('ta', 'gz'), moved(vector))  33.6 us
    pallas_call x3, Pallas kernels, contract(): pl.pallas_call(kernel, in_specs=[smem] + [anywhere] * (3 + nf) + [vmem] *...  27.4 us
    pallas_call x1, Pallas kernels, phase_blocks(): pl.pallas_call(phase_kernel, in_specs=[pl.BlockSpec(memory_space=pltpu.SM...  4.45 us
    unnamed x15, local copies, waits for them, and re-layouts  3.34 us
    ppermute x1, starting transfers between devices, body(): return (keep + lax.ppermute(send, 'gz', [(0, 1), (1, 0)]))[:, None]  2.83 us
    select_n x4, other arithmetic, pick(): value = jnp.where(index == i, sources[i], value)  2.8 us
  transfers between devices with their start and end apart: 22, of which 13 were waited for; matrix products, arithmetic and copies ran while one was open for 2% of the time, Pallas kernels for 17%

profile of v1, /device:TPU:1, one launch (start us, length us, event | category | flops | bytes accessed | tf_op | source)
XLA Modules:
  0.0 122.7 jit_solution(11734129675380961046)
XLA Ops:
  0.7 3.6 %collective-permute-start.3 = (f32[4,240,128]{2,1,0:T(8,128)}, f32[4,240,128]{2,1,0:T(8,128)S(1)}, u32[]{:S(2)}, u32[]{:S(2)}) collective-permute-start(f32[4,240,128]{2,1,0:T(8,128)} %get-tuple-element.29), channel_id=1, source_target_pairs={{0,8},{1,97},{2,10},{3,99},{4,12},{5,101},{6,14},{7,103},{8,16},{9... | collective-permute-start | bytes 1474568 | tf_op jit(solution)/shard_map/ppermute | solution.py:141
  4.4 3.8 %collective-permute-start.4 = (f32[4,240,128]{2,1,0:T(8,128)}, f32[4,240,128]{2,1,0:T(8,128)S(1)}, u32[]{:S(2)}, u32[]{:S(2)}) collective-permute-start(f32[4,240,128]{2,1,0:T(8,128)} %get-tuple-element.30), channel_id=1, source_target_pairs={{0,32},{1,7},{2,34},{3,1},{4,36},{5,3},{6,38},{7,5},{8,40},{9,15},... | collective-permute-start | bytes 1474568 | tf_op jit(solution)/shard_map/ppermute | solution.py:141
  8.1 2.5 %collective-permute-start.5 = (f32[4,240,128]{2,1,0:T(8,128)}, f32[4,240,128]{2,1,0:T(8,128)}, u32[]{:S(2)}, u32[]{:S(2)}) collective-permute-start(f32[4,240,128]{2,1,0:T(8,128)} %get-tuple-element.31), channel_id=1, source_target_pairs={{0,2},{1,25},{2,4},{3,27},{4,6},{5,29},{6,0},{7,31},{8,10},{9,1},{... | collective-permute-start | bytes 1474568 | tf_op jit(solution)/shard_map/ppermute | solution.py:141
  10.7 2.6 %collective-permute-start = (f32[4,320,128]{2,1,0:T(8,128)}, f32[4,320,128]{2,1,0:T(8,128)S(1)}, u32[]{:S(2)}, u32[]{:S(2)}) collective-permute-start(f32[4,320,128]{2,1,0:T(8,128)} %get-tuple-element.25), channel_id=1, source_target_pairs={{0,8},{1,97},{2,10},{3,99},{4,12},{5,101},{6,14},{7,103},{8,16},{9... | collective-permute-start | bytes 1966088 | tf_op jit(solution)/shard_map/ppermute | solution.py:141
  14.0 4.4 %phases.1 = (bf16[4,4,128,256]{3,2,1,0:T(8,128)(2,1)}, bf16[4,3,128,256]{3,2,1,0:T(8,128)(2,1)}) custom-call(s32[3]{0:T(128)} %source_ref.1, s32[27,3]{1,0:T(8,128)} %copy.9.momenta, f32[28,8,256]{2,1,0:T(8,128)} %constant.30.clone.places), custom_call_target="tpu_custom_call" | custom-call | tf_op jit(solution)/shard_map/phases/pallas_call | solution.py:464
  21.1 2.1 %collective-permute-done.1 = f32[4,320,128]{2,1,0:T(8,128)S(1)} collective-permute-done((f32[4,320,128]{2,1,0:T(8,128)}, f32[4,320,128]{2,1,0:T(8,128)S(1)}, u32[]{:S(2)}, u32[]{:S(2)}) %collective-permute-start.1) | collective-permute-done | bytes 655392 | tf_op jit(solution)/shard_map/ppermute | solution.py:141
  25.0 2.4 %collective-permute-start.8 = (f32[560,128]{1,0:T(8,128)S(1)}, f32[560,128]{1,0:T(8,128)S(1)}, u32[]{:S(2)}, u32[]{:S(2)}) collective-permute-start(f32[560,128]{1,0:T(8,128)S(1)} %pad_maximum_fusion.4), channel_id=1, source_target_pairs={{0,4},{1,17},{2,6},{3,19},{4,0},{5,21},{6,2},{7,23},{8,12},{9,25},... | collective-permute-start | bytes 860168 | tf_op jit(solution)/shard_map/ppermute | solution.py:141
  28.2 2.5 %collective-permute-start.6 = (f32[560,128]{1,0:T(8,128)S(1)}, f32[560,128]{1,0:T(8,128)S(1)}, u32[]{:S(2)}, u32[]{:S(2)}) collective-permute-start(f32[560,128]{1,0:T(8,128)S(1)} %pad_maximum_fusion.2), channel_id=1, source_target_pairs={{0,16},{1,65},{2,18},{3,67},{4,20},{5,69},{6,22},{7,71},{8,24},{9,... | collective-permute-start | bytes 860168 | tf_op jit(solution)/shard_map/ppermute | solution.py:141
  30.7 1.7 %collective-permute-done.8 = f32[560,128]{1,0:T(8,128)S(1)} collective-permute-done((f32[560,128]{1,0:T(8,128)S(1)}, f32[560,128]{1,0:T(8,128)S(1)}, u32[]{:S(2)}, u32[]{:S(2)}) %collective-permute-start.8) | collective-permute-done | bytes 286752 | tf_op jit(solution)/shard_map/ppermute | solution.py:141
  32.4 5.2 %collective-permute-done.7 = f32[560,128]{1,0:T(8,128)S(1)} collective-permute-done((f32[560,128]{1,0:T(8,128)S(1)}, f32[560,128]{1,0:T(8,128)S(1)}, u32[]{:S(2)}, u32[]{:S(2)}) %collective-permute-start.7) | collective-permute-done | bytes 286752 | tf_op jit(solution)/shard_map/ppermute | solution.py:141
  37.6 7.0 %collective-permute-start.10 = (f32[560,128]{1,0:T(8,128)S(1)}, f32[560,128]{1,0:T(8,128)S(1)}, u32[]{:S(2)}, u32[]{:S(2)}) collective-permute-start(f32[560,128]{1,0:T(8,128)S(1)} %maximum_select_fusion), channel_id=1, source_target_pairs={{0,84},{1,85},{2,86},{3,87},{4,80},{5,81},{6,82},{7,83},{8,92},{9,... | collective-permute-start | bytes 860168 | tf_op jit(solution)/shard_map/ppermute | solution.py:141
  44.7 6.9 %collective-permute-start.9 = (f32[560,128]{1,0:T(8,128)S(1)}, f32[560,128]{1,0:T(8,128)S(1)}, u32[]{:S(2)}, u32[]{:S(2)}) collective-permute-start(f32[560,128]{1,0:T(8,128)S(1)} %maximum_select_fusion), channel_id=1, source_target_pairs={{0,42},{1,127},{2,44},{3,121},{4,46},{5,123},{6,40},{7,125},{8,50}... | collective-permute-start | bytes 860168 | tf_op jit(solution)/shard_map/ppermute | solution.py:141
  51.6 10.7 %collective-permute-done.11 = f32[560,128]{1,0:T(8,128)S(1)} collective-permute-done((f32[560,128]{1,0:T(8,128)S(1)}, f32[560,128]{1,0:T(8,128)S(1)}, u32[]{:S(2)}, u32[]{:S(2)}) %collective-permute-start.11) | collective-permute-done | bytes 286752 | tf_op jit(solution)/shard_map/ppermute | solution.py:141
  62.5 1.6 %collective-permute-start.13 = (f32[560,128]{1,0:T(8,128)S(1)}, f32[560,128]{1,0:T(8,128)S(1)}, u32[]{:S(2)}, u32[]{:S(2)}) collective-permute-start(f32[560,128]{1,0:T(8,128)S(1)} %select_select_fusion), channel_id=1, source_target_pairs={{0,64},{1,5},{2,66},{3,7},{4,68},{5,1},{6,70},{7,3},{8,72},{9,13},... | collective-permute-start | bytes 860168 | tf_op jit(solution)/shard_map/ppermute | solution.py:141
  64.1 2.2 %collective-permute-start.12 = (f32[560,128]{1,0:T(8,128)S(1)}, f32[560,128]{1,0:T(8,128)S(1)}, u32[]{:S(2)}, u32[]{:S(2)}) collective-permute-start(f32[560,128]{1,0:T(8,128)S(1)} %select_select_fusion), channel_id=1, source_target_pairs={{0,16},{1,65},{2,18},{3,67},{4,20},{5,69},{6,22},{7,71},{8,24},{9,... | collective-permute-start | bytes 860168 | tf_op jit(solution)/shard_map/ppermute | solution.py:141
  66.3 3.5 %collective-permute-done.14 = f32[560,128]{1,0:T(8,128)S(1)} collective-permute-done((f32[560,128]{1,0:T(8,128)S(1)}, f32[560,128]{1,0:T(8,128)S(1)}, u32[]{:S(2)}, u32[]{:S(2)}) %collective-permute-start.14) | collective-permute-done | bytes 286752 | tf_op jit(solution)/shard_map/ppermute | solution.py:141
  70.2 2.7 %collective-permute-done.12 = f32[560,128]{1,0:T(8,128)S(1)} collective-permute-done((f32[560,128]{1,0:T(8,128)S(1)}, f32[560,128]{1,0:T(8,128)S(1)}, u32[]{:S(2)}, u32[]{:S(2)}) %collective-permute-start.12) | collective-permute-done | bytes 286752 | tf_op jit(solution)/shard_map/ppermute | solution.py:141
  73.0 3.7 %collective-permute-start.18 = (f32[4,240,128]{2,1,0:T(8,128)S(1)}, f32[4,240,128]{2,1,0:T(8,128)S(1)}, u32[]{:S(2)}, u32[]{:S(2)}) collective-permute-start(f32[4,240,128]{2,1,0:T(8,128)S(1)} %pad_maximum_fusion.1.refs_4_), channel_id=1, source_target_pairs={{0,8},{1,97},{2,10},{3,99},{4,12},{5,101},{6,14},{7,103},{8,16},{9... | collective-permute-start | bytes 1474568 | tf_op jit(solution)/shard_map/ppermute | solution.py:141
  80.8 1.6 %collective-permute-done.18.refs_5_ = f32[4,240,128]{2,1,0:T(8,128)S(1)} collective-permute-done((f32[4,240,128]{2,1,0:T(8,128)S(1)}, f32[4,240,128]{2,1,0:T(8,128)S(1)}, u32[]{:S(2)}, u32[]{:S(2)}) %collective-permute-start.18) | collective-permute-done | bytes 491552 | tf_op jit(solution)/shard_map/ppermute | solution.py:141
  84.3 5.0 %shard_map.85.refs_8_ = f32[64,128]{1,0:T(8,128)} custom-call(s32[1]{0:T(128)S(6)} %copy.11.refs_0_, f32[288,54,1,128]{3,2,1,0:T(1,128)} %bitcast.44, f32[288,54,1,128]{3,2,1,0:T(1,128)} %bitcast.47, bf16[4,4,128,256]{3,2,1,0:T(8,128)(2,1)} %get-tuple-element.22.refs_3_, f32[4,320,128]{2,1,0:T(8,128)} %copy-done), custom_call_target="tpu_custom_call" | custom-call | tf_op jit(solution)/shard_map/pallas_call | solution.py:380
  89.2 2.8 %collective-permute-done.19.refs_6_ = f32[4,240,128]{2,1,0:T(8,128)} collective-permute-done((f32[4,240,128]{2,1,0:T(8,128)S(1)}, f32[4,240,128]{2,1,0:T(8,128)}, u32[]{:S(2)}, u32[]{:S(2)}) %collective-permute-start.19) | collective-permute-done | bytes 491552 | tf_op jit(solution)/shard_map/ppermute | solution.py:141
  93.2 11.2 %shard_map.86.refs_7_ = f32[64,128]{1,0:T(8,128)} custom-call(s32[1]{0:T(128)S(6)} %copy.11.refs_0_, f32[288,54,1,128]{3,2,1,0:T(1,128)} %bitcast.45, f32[288,54,1,128]{3,2,1,0:T(1,128)} %bitcast.48, bf16[4,3,128,256]{3,2,1,0:T(8,128)(2,1)} %get-tuple-element.32.refs_3_, f32[4,240,128]{2,1,0:T(8,128)} %copy-done.1, f32[4,240,128]{2,1,0:T(8,128)} %copy-done.5, ...), custom_call_target="tpu_custom_call" | custom-call | tf_op jit(solution)/shard_map/pallas_call | solution.py:380
  106.3 11.2 %shard_map.87 = (f32[2,8,27]{2,1,0:T(8,128)}, f32[2,8,27]{2,1,0:T(8,128)}) custom-call(s32[1]{0:T(128)S(6)} %copy.11.refs_0_, f32[288,54,1,128]{3,2,1,0:T(1,128)} %bitcast.46, f32[288,54,1,128]{3,2,1,0:T(1,128)} %bitcast.49, bf16[4,4,128,256]{3,2,1,0:T(8,128)(2,1)} %get-tuple-element.22.refs_3_, f32[4,320,128]{2,1,0:T(8,128)} %copy-done.2, ...), custom_call_target="tpu_custom_call" | custom-call | tf_op jit(solution)/shard_map/pallas_call | solution.py:380
  117.5 2.8 %collective-permute-start.21 = (f32[2,8,27]{2,1,0:T(8,128)}, f32[2,8,27]{2,1,0:T(8,128)S(1)}, u32[]{:S(2)}, u32[]{:S(2)}) collective-permute-start(f32[2,8,27]{2,1,0:T(8,128)} %get-tuple-element.34), channel_id=1, source_target_pairs={{0,1},{1,0},{2,3},{3,2},{4,5},{5,4},{6,7},{7,6},{8,9},{9,8},{10,11... | collective-permute-start | bytes 5192 | tf_op jit(solution)/shard_map/ppermute | solution.py:490
  (60 shorter events, 18.2 us)
Async XLA Ops:
  0.7 12.6 %copy-start.6 = (s32[27,3]{0,1:T(4,128)S(1)}, s32[27,3]{0,1:T(4,128)}, u32[]{:S(2)}) copy-start(s32[27,3]{0,1:T(4,128)} %param.12) | copy-start | bytes 976
  0.7 12.5 %collective-permute-start.3 = (f32[4,240,128]{2,1,0:T(8,128)}, f32[4,240,128]{2,1,0:T(8,128)S(1)}, u32[]{:S(2)}, u32[]{:S(2)}) collective-permute-start(f32[4,240,128]{2,1,0:T(8,128)} %get-tuple-element.29), channel_id=1, source_target_pairs={{0,8},{1,97},{2,10},{3,99},{4,12},{5,101},{6,14},{7,103},{8,16},{9... | collective-permute-start | bytes 1474568 | tf_op jit(solution)/shard_map/ppermute | solution.py:141
  4.4 14.1 %collective-permute-start.4 = (f32[4,240,128]{2,1,0:T(8,128)}, f32[4,240,128]{2,1,0:T(8,128)S(1)}, u32[]{:S(2)}, u32[]{:S(2)}) collective-permute-start(f32[4,240,128]{2,1,0:T(8,128)} %get-tuple-element.30), channel_id=1, source_target_pairs={{0,32},{1,7},{2,34},{3,1},{4,36},{5,3},{6,38},{7,5},{8,40},{9,15},... | collective-permute-start | bytes 1474568 | tf_op jit(solution)/shard_map/ppermute | solution.py:141
  8.1 10.3 %collective-permute-start.5 = (f32[4,240,128]{2,1,0:T(8,128)}, f32[4,240,128]{2,1,0:T(8,128)}, u32[]{:S(2)}, u32[]{:S(2)}) collective-permute-start(f32[4,240,128]{2,1,0:T(8,128)} %get-tuple-element.31), channel_id=1, source_target_pairs={{0,2},{1,25},{2,4},{3,27},{4,6},{5,29},{6,0},{7,31},{8,10},{9,1},{... | collective-permute-start | bytes 1474568 | tf_op jit(solution)/shard_map/ppermute | solution.py:141
  10.7 10.4 %collective-permute-start = (f32[4,320,128]{2,1,0:T(8,128)}, f32[4,320,128]{2,1,0:T(8,128)S(1)}, u32[]{:S(2)}, u32[]{:S(2)}) collective-permute-start(f32[4,320,128]{2,1,0:T(8,128)} %get-tuple-element.25), channel_id=1, source_target_pairs={{0,8},{1,97},{2,10},{3,99},{4,12},{5,101},{6,14},{7,103},{8,16},{9... | collective-permute-start | bytes 1966088 | tf_op jit(solution)/shard_map/ppermute | solution.py:141
  13.2 9.9 %collective-permute-start.1 = (f32[4,320,128]{2,1,0:T(8,128)}, f32[4,320,128]{2,1,0:T(8,128)S(1)}, u32[]{:S(2)}, u32[]{:S(2)}) collective-permute-start(f32[4,320,128]{2,1,0:T(8,128)} %get-tuple-element.26), channel_id=1, source_target_pairs={{0,32},{1,7},{2,34},{3,1},{4,36},{5,3},{6,38},{7,5},{8,40},{9,15},... | collective-permute-start | bytes 1966088 | tf_op jit(solution)/shard_map/ppermute | solution.py:141
  13.2 10.5 %collective-permute-start.2 = (f32[4,320,128]{2,1,0:T(8,128)}, f32[4,320,128]{2,1,0:T(8,128)S(1)}, u32[]{:S(2)}, u32[]{:S(2)}) collective-permute-start(f32[4,320,128]{2,1,0:T(8,128)} %get-tuple-element.27), channel_id=1, source_target_pairs={{0,2},{1,25},{2,4},{3,27},{4,6},{5,29},{6,0},{7,31},{8,10},{9,1},{... | collective-permute-start | bytes 1966088 | tf_op jit(solution)/shard_map/ppermute | solution.py:141
  25.0 7.4 %collective-permute-start.8 = (f32[560,128]{1,0:T(8,128)S(1)}, f32[560,128]{1,0:T(8,128)S(1)}, u32[]{:S(2)}, u32[]{:S(2)}) collective-permute-start(f32[560,128]{1,0:T(8,128)S(1)} %pad_maximum_fusion.4), channel_id=1, source_target_pairs={{0,4},{1,17},{2,6},{3,19},{4,0},{5,21},{6,2},{7,23},{8,12},{9,25},... | collective-permute-start | bytes 860168 | tf_op jit(solution)/shard_map/ppermute | solution.py:141
  27.5 10.1 %collective-permute-start.7 = (f32[560,128]{1,0:T(8,128)S(1)}, f32[560,128]{1,0:T(8,128)S(1)}, u32[]{:S(2)}, u32[]{:S(2)}) collective-permute-start(f32[560,128]{1,0:T(8,128)S(1)} %pad_maximum_fusion.3), channel_id=1, source_target_pairs={{0,64},{1,5},{2,66},{3,7},{4,68},{5,1},{6,70},{7,3},{8,72},{9,13},... | collective-permute-start | bytes 860168 | tf_op jit(solution)/shard_map/ppermute | solution.py:141
  28.2 9.3 %collective-permute-start.6 = (f32[560,128]{1,0:T(8,128)S(1)}, f32[560,128]{1,0:T(8,128)S(1)}, u32[]{:S(2)}, u32[]{:S(2)}) collective-permute-start(f32[560,128]{1,0:T(8,128)S(1)} %pad_maximum_fusion.2), channel_id=1, source_target_pairs={{0,16},{1,65},{2,18},{3,67},{4,20},{5,69},{6,22},{7,71},{8,24},{9,... | collective-permute-start | bytes 860168 | tf_op jit(solution)/shard_map/ppermute | solution.py:141
  37.6 13.9 %collective-permute-start.10 = (f32[560,128]{1,0:T(8,128)S(1)}, f32[560,128]{1,0:T(8,128)S(1)}, u32[]{:S(2)}, u32[]{:S(2)}) collective-permute-start(f32[560,128]{1,0:T(8,128)S(1)} %maximum_select_fusion), channel_id=1, source_target_pairs={{0,84},{1,85},{2,86},{3,87},{4,80},{5,81},{6,82},{7,83},{8,92},{9,... | collective-permute-start | bytes 860168 | tf_op jit(solution)/shard_map/ppermute | solution.py:141
  44.7 17.6 %collective-permute-start.11 = (f32[560,128]{1,0:T(8,128)S(1)}, f32[560,128]{1,0:T(8,128)S(1)}, u32[]{:S(2)}, u32[]{:S(2)}) collective-permute-start(f32[560,128]{1,0:T(8,128)S(1)} %maximum_select_fusion), channel_id=1, source_target_pairs={{0,126},{1,43},{2,120},{3,45},{4,122},{5,47},{6,124},{7,41},{8,102... | collective-permute-start | bytes 860168 | tf_op jit(solution)/shard_map/ppermute | solution.py:141
  44.7 17.6 %collective-permute-start.9 = (f32[560,128]{1,0:T(8,128)S(1)}, f32[560,128]{1,0:T(8,128)S(1)}, u32[]{:S(2)}, u32[]{:S(2)}) collective-permute-start(f32[560,128]{1,0:T(8,128)S(1)} %maximum_select_fusion), channel_id=1, source_target_pairs={{0,42},{1,127},{2,44},{3,121},{4,46},{5,123},{6,40},{7,125},{8,50}... | collective-permute-start | bytes 860168 | tf_op jit(solution)/shard_map/ppermute | solution.py:141
  62.4 7.4 %collective-permute-start.14 = (f32[560,128]{1,0:T(8,128)S(1)}, f32[560,128]{1,0:T(8,128)S(1)}, u32[]{:S(2)}, u32[]{:S(2)}) collective-permute-start(f32[560,128]{1,0:T(8,128)S(1)} %select_select_fusion), channel_id=1, source_target_pairs={{0,4},{1,17},{2,6},{3,19},{4,0},{5,21},{6,2},{7,23},{8,12},{9,25},... | collective-permute-start | bytes 860168 | tf_op jit(solution)/shard_map/ppermute | solution.py:141
  62.5 7.7 %collective-permute-start.13 = (f32[560,128]{1,0:T(8,128)S(1)}, f32[560,128]{1,0:T(8,128)S(1)}, u32[]{:S(2)}, u32[]{:S(2)}) collective-permute-start(f32[560,128]{1,0:T(8,128)S(1)} %select_select_fusion), channel_id=1, source_target_pairs={{0,64},{1,5},{2,66},{3,7},{4,68},{5,1},{6,70},{7,3},{8,72},{9,13},... | collective-permute-start | bytes 860168 | tf_op jit(solution)/shard_map/ppermute | solution.py:141
  64.1 8.8 %collective-permute-start.12 = (f32[560,128]{1,0:T(8,128)S(1)}, f32[560,128]{1,0:T(8,128)S(1)}, u32[]{:S(2)}, u32[]{:S(2)}) collective-permute-start(f32[560,128]{1,0:T(8,128)S(1)} %select_select_fusion), channel_id=1, source_target_pairs={{0,16},{1,65},{2,18},{3,67},{4,20},{5,69},{6,22},{7,71},{8,24},{9,... | collective-permute-start | bytes 860168 | tf_op jit(solution)/shard_map/ppermute | solution.py:141
  73.0 16.3 %copy-start.1 = (f32[4,240,128]{2,1,0:T(8,128)}, f32[4,240,128]{2,1,0:T(8,128)S(1)}, u32[]{:S(2)}) copy-start(f32[4,240,128]{2,1,0:T(8,128)S(1)} %pad_maximum_fusion.1.refs_4_) | copy-start | bytes 1474564
  73.0 9.4 %collective-permute-start.18 = (f32[4,240,128]{2,1,0:T(8,128)S(1)}, f32[4,240,128]{2,1,0:T(8,128)S(1)}, u32[]{:S(2)}, u32[]{:S(2)}) collective-permute-start(f32[4,240,128]{2,1,0:T(8,128)S(1)} %pad_maximum_fusion.1.refs_4_), channel_id=1, source_target_pairs={{0,8},{1,97},{2,10},{3,99},{4,12},{5,101},{6,14},{7,103},{8,16},{9... | collective-permute-start | bytes 1474568 | tf_op jit(solution)/shard_map/ppermute | solution.py:141
  76.8 27.6 %collective-permute-start.15 = (f32[4,320,128]{2,1,0:T(8,128)S(1)}, f32[4,320,128]{2,1,0:T(8,128)S(1)}, u32[]{:S(2)}, u32[]{:S(2)}) collective-permute-start(f32[4,320,128]{2,1,0:T(8,128)S(1)} %pad_maximum_fusion.refs_4_), channel_id=1, source_target_pairs={{0,8},{1,97},{2,10},{3,99},{4,12},{5,101},{6,14},{7,103},{8,16},{9... | collective-permute-start | bytes 1966088 | tf_op jit(solution)/shard_map/ppermute | solution.py:141
  76.8 27.6 %collective-permute-start.16 = (f32[4,320,128]{2,1,0:T(8,128)S(1)}, f32[4,320,128]{2,1,0:T(8,128)S(1)}, u32[]{:S(2)}, u32[]{:S(2)}) collective-permute-start(f32[4,320,128]{2,1,0:T(8,128)S(1)} %pad_maximum_fusion.refs_4_), channel_id=1, source_target_pairs={{0,32},{1,7},{2,34},{3,1},{4,36},{5,3},{6,38},{7,5},{8,40},{9,15},... | collective-permute-start | bytes 1966088 | tf_op jit(solution)/shard_map/ppermute | solution.py:141
  78.1 26.4 %collective-permute-start.17 = (f32[4,320,128]{2,1,0:T(8,128)S(1)}, f32[4,320,128]{2,1,0:T(8,128)S(1)}, u32[]{:S(2)}, u32[]{:S(2)}) collective-permute-start(f32[4,320,128]{2,1,0:T(8,128)S(1)} %pad_maximum_fusion.refs_4_), channel_id=1, source_target_pairs={{0,2},{1,25},{2,4},{3,27},{4,6},{5,29},{6,0},{7,31},{8,10},{9,1},{... | collective-permute-start | bytes 1966088 | tf_op jit(solution)/shard_map/ppermute | solution.py:141
  79.4 12.6 %collective-permute-start.19 = (f32[4,240,128]{2,1,0:T(8,128)S(1)}, f32[4,240,128]{2,1,0:T(8,128)}, u32[]{:S(2)}, u32[]{:S(2)}) collective-permute-start(f32[4,240,128]{2,1,0:T(8,128)S(1)} %pad_maximum_fusion.1.refs_4_), channel_id=1, source_target_pairs={{0,32},{1,7},{2,34},{3,1},{4,36},{5,3},{6,38},{7,5},{8,40},{9,15},... | collective-permute-start | bytes 1474568 | tf_op jit(solution)/shard_map/ppermute | solution.py:141
  83.2 10.0 %collective-permute-start.20 = (f32[4,240,128]{2,1,0:T(8,128)S(1)}, f32[4,240,128]{2,1,0:T(8,128)}, u32[]{:S(2)}, u32[]{:S(2)}) collective-permute-start(f32[4,240,128]{2,1,0:T(8,128)S(1)} %pad_maximum_fusion.1.refs_4_), channel_id=1, source_target_pairs={{0,2},{1,25},{2,4},{3,27},{4,6},{5,29},{6,0},{7,31},{8,10},{9,1},{... | collective-permute-start | bytes 1474568 | tf_op jit(solution)/shard_map/ppermute | solution.py:141
  117.5 3.9 %collective-permute-start.21 = (f32[2,8,27]{2,1,0:T(8,128)}, f32[2,8,27]{2,1,0:T(8,128)S(1)}, u32[]{:S(2)}, u32[]{:S(2)}) collective-permute-start(f32[2,8,27]{2,1,0:T(8,128)} %get-tuple-element.34), channel_id=1, source_target_pairs={{0,1},{1,0},{2,3},{3,2},{4,5},{5,4},{6,7},{7,6},{8,9},{9,8},{10,11... | collective-permute-start | bytes 5192 | tf_op jit(solution)/shard_map/ppermute | solution.py:490
  (5 other events, 11.0 us)
